TPU v7x, 32 devices: a whole 2x2x4 slice. The times are simulated.
32 devices in a mesh: coil: 8 (over z, x), frame: 4 (over y, core).
Axes of the slice: x: 2, y: 2, z: 4, core: 2. Of those that a mesh axis runs over, the one named last changes fastest.
Arguments:
- initial_image: float32 [256, 4, 2, 256], P('coil', 'frame'), may hold values from -3 to 3
- coil_maps: bfloat16 [8, 2, 256, 256], P('coil'), may hold values from -2 to 2
- samples: bfloat16 [8, 4, 18, 2, 256], P('coil', 'frame'), may hold values from -6 to 6
- blocks_used: int32 [4], P('frame'), may hold values from 1 to 18, 37 in all
- row_offset: int32 [4, 18], P('frame'), may hold values from 0 to 128
- col_offset: int32 [4, 18], P('frame'), may hold values from 0 to 128
- row_first: int32 [4, 18, 256], P('frame'), may hold values from 0 to 124
- col_first: int32 [4, 18, 256], P('frame'), may hold values from 0 to 124
- row_taps: bfloat16 [4, 18, 4, 256], P('frame'), may hold values from 0.099609375 to 0.59765625
- col_taps: bfloat16 [4, 18, 4, 256], P('frame'), may hold values from 0.099609375 to 0.59765625
Outputs:
- image: float32 [256, 4, 2, 256], P('coil', 'frame')
- misfit: float32 [2, 4], P(None, 'frame')
Inputs may be any that keep to these rules, and one draw needn't show every extreme that they name: Blocks 0 to blocks_used minus one of the frame were acquired. `row_first`: the kernel's 4 rows lie inside the tile. `col_first`: the kernel's 4 columns lie inside the tile.
All inputs are finite; a program needn't handle non-finite values.
Results may differ from a plain program's by a relative error of at most 0.006.
Values may be sent and summed in bfloat16 or wider, within the bound.
A program may use at most 64 MiB of HBM per device.

v0:
```python
import functools
import math

import jax
import jax.numpy as jnp
import ml_dtypes
import numpy as np
from jax import lax
from jax.experimental import pallas as pl
from jax.experimental.pallas import tpu as pltpu
from jax.sharding import PartitionSpec as P

ITERS = 2
GROUP = 6
LANES = 128

step_size = 2.0
tv_weight = 0.1
smooth_floor = 0.5
shrink_weight = 0.1

F32 = jnp.float32
BF16 = jnp.bfloat16
MESH = pl.DeviceIdType.MESH


def table_pair(order):
    counter = np.arange(order)
    angle = (counter[:, None] * counter[None, :] % order) * (2.0 * math.pi / order)
    cosine = (np.cos(angle) / math.sqrt(order)).astype(ml_dtypes.bfloat16)
    sine = (np.sin(angle) / math.sqrt(order)).astype(ml_dtypes.bfloat16)
    return np.concatenate([cosine, sine], axis=1)


def partner_of(place, k, count):
    if count & (count - 1):
        return lax.rem(place + k, count)
    result, bit = 0, 1
    while bit < count:
        digit = place // bit % 2
        result = result + (1 - digit if k & bit else digit) * bit
        bit *= 2
    return result


def owner_of(place, k, count):
    if count & (count - 1):
        return lax.rem(place + count - k, count)
    return partner_of(place, k, count)


def dot(left, right):
    return jnp.dot(left, right, preferred_element_type=F32)


def dot_nt(left, right):
    return lax.dot_general(left, right, (((1,), (1,)), ((), ())), preferred_element_type=F32)


def partner(values, axis, parity):
    size = values.shape[axis]
    return jnp.where(
        parity == 0, pltpu.roll(values, size - 1, axis), pltpu.roll(values, 1, axis)
    )


def shrink_pair(real, imag, limit):
    length = jnp.sqrt(real * real + imag * imag)
    factor = jnp.maximum(length - limit, 0.0) / jnp.maximum(length, limit)
    return real * factor, imag * factor


def wavelet_prox(fields, limit):
    shape = fields[0].shape
    row_parity = lax.broadcasted_iota(jnp.int32, shape, 0) % 2
    col_parity = lax.broadcasted_iota(jnp.int32, shape, 1) % 2
    row_sign = jnp.where(row_parity == 0, 1.0, -1.0)
    col_sign = jnp.where(col_parity == 0, 1.0, -1.0)
    parts = []
    for field in fields:
        beside = partner(field, 1, col_parity)
        col_sum = field + beside
        col_diff = (field - beside) * col_sign
        sum_below = partner(col_sum, 0, row_parity)
        diff_below = partner(col_diff, 0, row_parity)
        approx = (col_sum + sum_below) * 0.5
        horiz = (col_diff + diff_below) * 0.5
        vertical = (col_sum - sum_below) * row_sign * 0.5
        diagonal = (col_diff - diff_below) * row_sign * 0.5
        parts.append((approx, horiz, vertical, diagonal))
    real, imag = parts
    horiz = shrink_pair(real[1], imag[1], limit)
    vertical = shrink_pair(real[2], imag[2], limit)
    diagonal = shrink_pair(real[3], imag[3], limit)
    return [
        (parts[p][0] + col_sign * horiz[p] + row_sign * vertical[p] + row_sign * col_sign * diagonal[p])
        for p in range(2)
    ]


def kernel(
    coils,
    frames,
    *refs,
):
    inputs = refs[:11]
    image_ref, misfit_ref = refs[11:13]
    held = refs[13:24]
    input_sem = refs[24]
    loads = []
    for place, (source, target) in enumerate(zip(inputs, held)):
        copy = pltpu.make_async_copy(source, target, input_sem.at[place])
        copy.start()
        loads.append(copy)
    run(coils, frames, loads, *held, image_ref, misfit_ref, *refs[25:])


def run(
    coils,
    frames,
    loads,
    start_ref,
    maps_ref,
    samples_ref,
    used_ref,
    row_off_ref,
    col_off_ref,
    row_first_ref,
    col_first_ref,
    row_taps_ref,
    col_taps_ref,
    table_ref,
    image_ref,
    misfit_ref,
    forward_ref,
    inverse_ref,
    row_ref,
    col_ref,
    stack_ref,
    space_ref,
    grid_ref,
    grad_ref,
    moving_ref,
    current_ref,
    low_ref,
    gather_ref,
    outgo_ref,
    income_ref,
    beside_ref,
    tally_ref,
    tallies_ref,
    gather_send,
    gather_recv,
    income_send,
    income_recv,
    beside_send,
    beside_recv,
    tally_send,
    tally_recv,
):
    coil = lax.axis_index("coil")
    frame = lax.axis_index("frame")
    size = maps_ref.shape[2]
    blocks = samples_ref.shape[2]
    spoke = samples_ref.shape[4]
    taps = row_taps_ref.shape[2]
    rows = size // coils
    later = lax.rem(frame + 1, frames)
    earlier = lax.rem(frame + frames - 1, frames)
    peers = [partner_of(coil, k, coils) for k in range(coils)]
    owners = [owner_of(coil, k, coils) for k in range(coils)]
    order = list(range(coils - 1, 0, -1))
    wire = gather_ref.dtype

    barrier = pltpu.get_barrier_semaphore()
    for k in range(1, coils):
        pl.semaphore_signal(barrier, inc=1, device_id={"coil": peers[k]}, device_id_type=MESH)
    for nearby in (later, earlier):
        pl.semaphore_signal(barrier, inc=1, device_id={"frame": nearby}, device_id_type=MESH)
    loads[0].wait()
    for p in range(2):
        value = start_ref[:, 0, p, :]
        low_ref[0, p] = value.astype(BF16).astype(wire)
        moving_ref[0, p] = value
        current_ref[p] = value
    pl.semaphore_wait(barrier, coils - 1 + 2)

    pending = []

    def send(source, target, send_sem, recv_sem, where):
        copy = pltpu.make_async_remote_copy(
            src_ref=source,
            dst_ref=target,
            send_sem=send_sem,
            recv_sem=recv_sem,
            device_id=where,
            device_id_type=MESH,
        )
        copy.start()
        pending.append(copy)
        return copy

    def spread_image(it, low, full):
        gathers = {
            k: send(low, gather_ref.at[it, k], gather_send.at[it, k], gather_recv.at[it, k], {"coil": peers[k]})
            for k in order
        }
        besides = [
            send(full, beside_ref.at[it, side], beside_send.at[it, side], beside_recv.at[it, side], {"frame": where})
            for side, where in ((0, later), (1, earlier))
        ]
        return gathers, besides

    gathers, besides = spread_image(0, low_ref.at[0], moving_ref.at[0])

    for place in range(4, 10):
        loads[place].wait()
    loads[10].wait()
    cosine = table_ref[:, :size]
    sine = table_ref[:, size:]
    forward_ref[:size, :size] = cosine
    forward_ref[:size, size:] = -sine
    forward_ref[size:, :size] = sine
    forward_ref[size:, size:] = cosine
    inverse_ref[:size, :size] = cosine
    inverse_ref[:size, size:] = sine
    inverse_ref[size:, :size] = -sine
    inverse_ref[size:, size:] = cosine

    strip = 64
    group = max(d for d in range(1, GROUP + 1) if blocks % d == 0)

    def build(block, carry):
        for first_ref, off_ref, taps_ref, into_ref in (
            (row_first_ref, row_off_ref, row_taps_ref, row_ref),
            (col_first_ref, col_off_ref, col_taps_ref, col_ref),
        ):
            first = first_ref[block] + off_ref[0, block]
            weights = taps_ref[0, block].astype(F32)
            for low in range(0, size, strip):
                distance = lax.broadcasted_iota(jnp.int32, (strip, spoke), 0) + low - first
                matrix = jnp.zeros((strip, spoke), F32)
                for tap in range(taps):
                    matrix = jnp.where(distance == tap, weights[tap : tap + 1], matrix)
                into_ref[block, low : low + strip, :] = matrix.astype(BF16)
        return carry

    lax.fori_loop(0, blocks, build, 0)
    tally_ref[...] = jnp.zeros_like(tally_ref)
    for place in range(1, 4):
        loads[place].wait()
    used = used_ref[0, 0]
    momentum = 1.0

    for it in range(ITERS):
        for k in [0] + order[::-1]:
            if k == 0:
                piece = low_ref[it]
            else:
                gathers[k].wait_recv()
                piece = gather_ref[it, k]
            piece = piece.astype(F32)
            owner = owners[k]
            at = pl.multiple_of(owner * rows, rows)
            at_below = pl.multiple_of(owner * rows + size, rows)
            map_real = maps_ref[0, 0, pl.ds(at, rows), :].astype(F32)
            map_imag = maps_ref[0, 1, pl.ds(at, rows), :].astype(F32)
            real = (map_real * piece[0] - map_imag * piece[1]).astype(BF16).astype(wire)
            imag = (map_real * piece[1] + map_imag * piece[0]).astype(BF16).astype(wire)
            stack_ref[pl.ds(at, rows), :size] = real
            stack_ref[pl.ds(at, rows), size:] = imag
            stack_ref[pl.ds(at_below, rows), :size] = imag
            stack_ref[pl.ds(at_below, rows), size:] = -real
        half = dot(table_ref[...], stack_ref[...].astype(BF16)).astype(BF16)
        kspace = dot(half, forward_ref[...]).astype(BF16)
        space_ref[:size] = kspace[:, :size]
        space_ref[size:] = kspace[:, size:]
        grid_ref[...] = jnp.zeros_like(grid_ref)

        def visit(turn, total):
            weighted = ([], [])
            sides = []
            for member in range(group):
                block = turn * group + member
                cols = col_ref[block]
                sides.append(cols)
                rows_wide = row_ref[block].astype(F32)
                across = dot(space_ref[...], cols)
                measured = samples_ref[0, 0, block].astype(F32)
                active = jnp.where(block < used, 1.0, 0.0)
                for p in range(2):
                    predicted = jnp.sum(
                        across[p * size : (p + 1) * size] * rows_wide, axis=0, keepdims=True
                    )
                    resid = (predicted - measured[p : p + 1]) * active
                    total = total + resid * resid
                    resid_low = resid.astype(BF16).astype(F32)
                    weighted[p].append((resid_low * rows_wide).astype(BF16))
            both = jnp.concatenate([jnp.concatenate(part, axis=1) for part in weighted], axis=0)
            grid_ref[...] += dot_nt(both, jnp.concatenate(sides, axis=1))
            return total

        total = lax.fori_loop(0, blocks // group, visit, jnp.zeros((1, spoke), F32))
        tally_ref[it : it + 1, :] = total
        tally_copies = []
        if it == ITERS - 1:
            tally_copies = [
                send(tally_ref, tallies_ref.at[k], tally_send.at[k], tally_recv.at[k], {"coil": peers[k]})
                for k in range(1, coils)
            ]
        grid_real = grid_ref[:size].astype(BF16)
        grid_imag = grid_ref[size:].astype(BF16)
        turned = jnp.concatenate(
            [
                jnp.concatenate([grid_real, grid_imag], axis=1),
                jnp.concatenate([-grid_imag, grid_real], axis=1),
            ],
            axis=0,
        )
        back_half = dot(table_ref[...], turned).astype(BF16)
        coil_back = dot(back_half, inverse_ref[...])
        map_real = maps_ref[0, 0].astype(F32)
        map_imag = maps_ref[0, 1].astype(F32)
        back_real = coil_back[:, :size]
        back_imag = coil_back[:, size:]
        real = map_real * back_real + map_imag * back_imag
        imag = map_real * back_imag - map_imag * back_real
        outgo_ref[it, 0] = real.astype(wire)
        outgo_ref[it, 1] = imag.astype(wire)
        incomes = {}
        for k in order:
            at = pl.multiple_of(peers[k] * rows, rows)
            incomes[k] = send(
                outgo_ref.at[it, :, pl.ds(at, rows), :],
                income_ref.at[it, k],
                income_send.at[it, k],
                income_recv.at[it, k],
                {"coil": peers[k]},
            )
        grad_ref[0] = real
        grad_ref[1] = imag

        for copy in besides:
            copy.wait_recv()
        moving = [moving_ref[it, p] for p in range(2)]
        ahead = [beside_ref[it, 1, p] - moving[p] for p in range(2)]
        behind = [moving[p] - beside_ref[it, 0, p] for p in range(2)]
        floor = smooth_floor * smooth_floor
        ahead_length = jnp.sqrt(ahead[0] * ahead[0] + ahead[1] * ahead[1] + floor)
        behind_length = jnp.sqrt(behind[0] * behind[0] + behind[1] * behind[1] + floor)
        variation = [behind[p] / behind_length - ahead[p] / ahead_length for p in range(2)]

        here = pl.multiple_of(coil * rows, rows)
        sums = [grad_ref[p, pl.ds(here, rows), :] for p in range(2)]
        for k in range(1, coils):
            incomes[k].wait_recv()
            sums = [sums[p] + income_ref[it, k, p].astype(F32) for p in range(2)]
        descent = [moving[p] - step_size * (sums[p] + tv_weight * variation[p]) for p in range(2)]
        doubled = wavelet_prox(descent, step_size * shrink_weight)
        updated = [doubled[p] * 0.5 for p in range(2)]
        following = (1.0 + math.sqrt(1.0 + 4.0 * momentum * momentum)) / 2.0
        if it == ITERS - 1:
            tiles = size // LANES
            for p in range(2):
                for tile in range(tiles):
                    image_ref[pl.ds(2 * tile + p, rows, stride=2 * tiles), :] = doubled[p][
                        :, tile * LANES : (tile + 1) * LANES
                    ]
        else:
            factor = (momentum - 1.0) / following
            for p in range(2):
                ahead_value = updated[p]
                if factor != 0.0:
                    ahead_value = ahead_value + factor * (updated[p] - current_ref[p])
                low_ref[it + 1, p] = ahead_value.astype(BF16).astype(wire)
                moving_ref[it + 1, p] = ahead_value
                current_ref[p] = updated[p]
            gathers, besides = spread_image(it + 1, low_ref.at[it + 1], moving_ref.at[it + 1])
        momentum = following

    tally = tally_ref[...]
    for k in range(1, coils):
        tally_copies[k - 1].wait_recv()
        tally = tally + tallies_ref[k]
    lane = lax.broadcasted_iota(jnp.int32, (1, ITERS), 1)
    misfit = jnp.zeros((1, ITERS), F32)
    for it in range(ITERS):
        misfit = jnp.where(lane == it, jnp.sum(tally[it : it + 1], axis=1, keepdims=True), misfit)
    misfit_ref[...] = misfit
    for copy in pending:
        copy.wait_send()


def on_device(coils, frames, table, image, coil_maps, samples, blocks_used, row_off, col_off, row_first, col_first, *taps):
    size = coil_maps.shape[3]
    blocks = samples.shape[2]
    spoke = samples.shape[4]
    rows = size // coils
    wire = BF16 if rows % 16 == 0 else F32
    row_first = jnp.transpose(row_first, (1, 0, 2))
    col_first = jnp.transpose(col_first, (1, 0, 2))
    vmem = pl.BlockSpec(memory_space=pltpu.VMEM)
    operands = (
        image,
        coil_maps,
        samples,
        blocks_used.reshape(1, 1),
        row_off,
        col_off,
        row_first,
        col_first,
        *taps,
        table,
    )
    scalars = (3, 4, 5)
    held = [
        (pltpu.SMEM if place in scalars else pltpu.VMEM)(operand.shape, operand.dtype)
        for place, operand in enumerate(operands)
    ]
    shard = (2, rows, size)
    dma = pltpu.SemaphoreType.DMA
    doubled, misfit = pl.pallas_call(
        functools.partial(kernel, coils, frames),
        out_shape=(
            jax.ShapeDtypeStruct((2 * rows * size // LANES, LANES), F32),
            jax.ShapeDtypeStruct((1, ITERS), F32),
        ),
        in_specs=[pl.BlockSpec(memory_space=pl.ANY)] * len(operands),
        out_specs=(vmem, vmem),
        scratch_shapes=held
        + [
            dma((len(operands),)),
            pltpu.VMEM((2 * size, 2 * size), BF16),
            pltpu.VMEM((2 * size, 2 * size), BF16),
            pltpu.VMEM((blocks, size, spoke), BF16),
            pltpu.VMEM((blocks, size, spoke), BF16),
            pltpu.VMEM((2 * size, 2 * size), wire),
            pltpu.VMEM((2 * size, size), BF16),
            pltpu.VMEM((2 * size, size), F32),
            pltpu.VMEM((2, size, size), F32),
            pltpu.VMEM((ITERS,) + shard, F32),
            pltpu.VMEM(shard, F32),
            pltpu.VMEM((ITERS,) + shard, wire),
            pltpu.VMEM((ITERS, coils) + shard, wire),
            pltpu.VMEM((ITERS, 2, size, size), wire),
            pltpu.VMEM((ITERS, coils) + shard, wire),
            pltpu.VMEM((ITERS, 2) + shard, F32),
            pltpu.VMEM((8, spoke), F32),
            pltpu.VMEM((coils, 8, spoke), F32),
            dma((ITERS, coils)),
            dma((ITERS, coils)),
            dma((ITERS, coils)),
            dma((ITERS, coils)),
            dma((ITERS, 2)),
            dma((ITERS, 2)),
            dma((coils,)),
            dma((coils,)),
        ],
        compiler_params=pltpu.CompilerParams(
            collective_id=0, has_side_effects=True, vmem_limit_bytes=56 * 1024 * 1024
        ),
    )(*operands)
    updated = (doubled * 0.5).reshape(rows, size // LANES, 2, LANES).transpose(0, 2, 1, 3)
    scale = 0.5 / (coils * blocks * spoke)
    return updated.reshape(image.shape), jnp.transpose(misfit * scale)


def solution(mesh):
    placed = (
        P("coil", "frame", None, None),
        P("coil", None, None, None),
        P("coil", "frame", None, None, None),
        P("frame"),
        P("frame", None),
        P("frame", None),
        P("frame", None, None),
        P("frame", None, None),
        P("frame", None, None, None),
        P("frame", None, None, None),
    )

    def run(*args):
        table = jnp.asarray(table_pair(args[1].shape[3]))
        body = functools.partial(on_device, mesh.shape["coil"], mesh.shape["frame"], table)
        return jax.shard_map(
            body,
            mesh=mesh,
            in_specs=placed,
            out_specs=(P("coil", "frame", None, None), P(None, "frame")),
            check_vma=False,
        )(*args)

    return run
```

profile of v0, /device:TPU:0, one launch (start us, length us, event | category | flops | bytes accessed | tf_op | source)
XLA Modules:
  0.0 47.6 jit_solution(10973187777622177751)
XLA Ops:
  1.3 43.7 %shard_map.122 = (f32[128,128]{1,0:T(8,128)}, f32[1,2]{1,0:T(1,128)}) custom-call(f32[32,1,2,256]{3,2,1,0:T(2,128)} %refs_0_.1, bf16[1,2,256,256]{3,2,1,0:T(8,128)(2,1)} %refs_1_.1, bf16[1,1,18,2,256]{4,3,2,1,0:T(2,128)(2,1)} %refs_2_.1, s32[1,1]{1,0:T(1,128)} %bitcast.10.refs_3_, s32[1,18]{1,0:T(1,128)} %refs_4_.1, s32[1,18]{1,0:T(1,128)} %refs_5_.1, ...), custom_call_target="tpu_custom_call" | custom-call | tf_op jit(solution)/shard_map/pallas_call | solution.py:422
  45.0 1.5 %broadcast_multiply_fusion = f32[128,128]{1,0:T(8,128)} fusion(f32[128,128]{1,0:T(8,128)} %get-tuple-element.4), kind=kLoop, calls=%fused_computation | loop fusion | flops 16384 | bytes 131072 | tf_op jit(solution)/shard_map/mul | solution.py:463
  46.5 0.0 copy-start
  46.5 0.6 %copy-done = f32[1,2]{1,0:T(1,128)S(1)} copy-done((f32[1,2]{1,0:T(1,128)S(1)}, f32[1,2]{1,0:T(1,128)}, u32[]{:S(2)}) %copy-start) | copy-done | bytes 32
  47.1 0.5 %multiply_bitcast_fusion = f32[2,1]{0,1:T(1,128)} fusion(f32[1,2]{1,0:T(1,128)S(1)} %copy-done), kind=kLoop, calls=%fused_computation.1 | loop fusion | flops 2 | bytes 16 | tf_op jit(solution)/shard_map/transpose | solution.py:465
Async XLA Ops:
  46.5 0.6 %copy-start = (f32[1,2]{1,0:T(1,128)S(1)}, f32[1,2]{1,0:T(1,128)}, u32[]{:S(2)}) copy-start(f32[1,2]{1,0:T(1,128)} %get-tuple-element.5) | copy-start | bytes 28
where the time goes:
time: 47.8 us; the launch traced here: 47.6 us
  Pallas kernels  43.7 us (91%)
  other arithmetic  1.99 us (4%)
  between operations  1.29 us (3%)
  local copies, waits for them, and re-layouts  0.6 us (1%)
    pallas_call x1, Pallas kernels, on_device(): pl.pallas_call(functools.partial(kernel, coils, frames), out_shape=(jax.S...  43.7 us
    mul x1, other arithmetic, on_device(): doubled * 0.5  1.48 us

commit v1 on v0

--- a/solution.py
+++ b/solution.py
@@ -11,7 +11,9 @@
 from jax.sharding import PartitionSpec as P
 
 ITERS = 2
-GROUP = 6
+GROUP = 18
+TILE = 128
+ALIGN = 16
 LANES = 128
 
 step_size = 2.0
@@ -228,6 +230,7 @@
     inverse_ref[size:, size:] = cosine
 
     strip = 64
+    strips = size // ALIGN
     group = max(d for d in range(1, GROUP + 1) if blocks % d == 0)
 
     def build(block, carry):
@@ -242,11 +245,20 @@
                 matrix = jnp.zeros((strip, spoke), F32)
                 for tap in range(taps):
                     matrix = jnp.where(distance == tap, weights[tap : tap + 1], matrix)
-                into_ref[block, low : low + strip, :] = matrix.astype(BF16)
+                matrix = matrix.astype(BF16)
+                if into_ref is col_ref:
+                    into_ref[block, low : low + strip, :] = matrix
+                else:
+                    into_ref[block, low // ALIGN : (low + strip) // ALIGN] = matrix.reshape(-1, ALIGN, spoke)
+        row_ref[block, strips] = jnp.zeros((ALIGN, spoke), BF16)
         return carry
 
     lax.fori_loop(0, blocks, build, 0)
     tally_ref[...] = jnp.zeros_like(tally_ref)
+    for p in range(2):
+        space_ref[p, strips] = jnp.zeros((ALIGN, size), BF16)
+    window = TILE // ALIGN + 1
+    deep = window * ALIGN
     for place in range(1, 4):
         loads[place].wait()
     used = used_ref[0, 0]
@@ -273,34 +285,49 @@
             stack_ref[pl.ds(at_below, rows), size:] = -real
         half = dot(table_ref[...], stack_ref[...].astype(BF16)).astype(BF16)
         kspace = dot(half, forward_ref[...]).astype(BF16)
-        space_ref[:size] = kspace[:, :size]
-        space_ref[size:] = kspace[:, size:]
+        for p in range(2):
+            space_ref[p, :strips] = kspace[:, p * size : (p + 1) * size].reshape(strips, ALIGN, size)
         grid_ref[...] = jnp.zeros_like(grid_ref)
 
-        def visit(turn, total):
-            weighted = ([], [])
-            sides = []
+        def predict(turn, total):
+            lows = []
             for member in range(group):
                 block = turn * group + member
-                cols = col_ref[block]
-                sides.append(cols)
-                rows_wide = row_ref[block].astype(F32)
-                across = dot(space_ref[...], cols)
+                at = lax.div(row_off_ref[0, block], ALIGN)
+                near = jnp.concatenate([space_ref[p, at + i] for p in range(2) for i in range(window)], axis=0)
+                across = dot(near, col_ref[block])
+                rows_wide = jnp.concatenate([row_ref[block, at + i] for i in range(window)], axis=0).astype(F32)
                 measured = samples_ref[0, 0, block].astype(F32)
                 active = jnp.where(block < used, 1.0, 0.0)
                 for p in range(2):
                     predicted = jnp.sum(
-                        across[p * size : (p + 1) * size] * rows_wide, axis=0, keepdims=True
+                        across[p * deep : (p + 1) * deep] * rows_wide, axis=0, keepdims=True
                     )
                     resid = (predicted - measured[p : p + 1]) * active
                     total = total + resid * resid
-                    resid_low = resid.astype(BF16).astype(F32)
-                    weighted[p].append((resid_low * rows_wide).astype(BF16))
-            both = jnp.concatenate([jnp.concatenate(part, axis=1) for part in weighted], axis=0)
+                    lows.append(resid)
+            return total, tuple(lows)
+
+        def spread(turn, lows):
+            left, sides = ([], []), []
+            for member in range(group):
+                block = turn * group + member
+                sides.append(col_ref[block])
+                rows_wide = row_ref[block, :strips].reshape(size, spoke)
+                for p in range(2):
+                    left[p].append(lows[2 * member + p].astype(BF16) * rows_wide)
+            both = jnp.concatenate([jnp.concatenate(part, axis=1) for part in left], axis=0)
             grid_ref[...] += dot_nt(both, jnp.concatenate(sides, axis=1))
-            return total
-
-        total = lax.fori_loop(0, blocks // group, visit, jnp.zeros((1, spoke), F32))
+
+        def visit(turn, carry):
+            total, lows = carry
+            spread(turn - 1, lows)
+            return predict(turn, total)
+
+        turns = blocks // group
+        carry = predict(0, jnp.zeros((1, spoke), F32))
+        total, lows = lax.fori_loop(1, turns, visit, carry) if turns > 1 else carry
+        spread(turns - 1, lows)
         tally_ref[it : it + 1, :] = total
         tally_copies = []
         if it == ITERS - 1:
@@ -422,8 +449,8 @@
     doubled, misfit = pl.pallas_call(
         functools.partial(kernel, coils, frames),
         out_shape=(
-            jax.ShapeDtypeStruct((2 * rows * size // LANES, LANES), F32),
-            jax.ShapeDtypeStruct((1, ITERS), F32),
+            pltpu.VMEM((2 * rows * size // LANES, LANES), F32),
+            pltpu.VMEM((1, ITERS), F32),
         ),
         in_specs=[pl.BlockSpec(memory_space=pl.ANY)] * len(operands),
         out_specs=(vmem, vmem),
@@ -432,10 +459,10 @@
             dma((len(operands),)),
             pltpu.VMEM((2 * size, 2 * size), BF16),
             pltpu.VMEM((2 * size, 2 * size), BF16),
-            pltpu.VMEM((blocks, size, spoke), BF16),
+            pltpu.VMEM((blocks, size // ALIGN + 1, ALIGN, spoke), BF16),
             pltpu.VMEM((blocks, size, spoke), BF16),
             pltpu.VMEM((2 * size, 2 * size), wire),
-            pltpu.VMEM((2 * size, size), BF16),
+            pltpu.VMEM((2, size // ALIGN + 1, ALIGN, size), BF16),
             pltpu.VMEM((2 * size, size), F32),
             pltpu.VMEM((2, size, size), F32),
             pltpu.VMEM((ITERS,) + shard, F32),

time: 47.8 us -> 43.9 us (0.918)
  Pallas kernels: 43.7 us -> 41.3 us
  other arithmetic: 1.99 us -> 1.15 us
  local copies, waits for them, and re-layouts: 0.6 us -> 0 us
    pallas_call x1, Pallas kernels: 43.7 us -> 41.3 us  [on_device(): pl.pallas_call(functools.partial(kernel, coils, frames), out_shape=(pltpu...]
    mul x1, other arithmetic: 1.48 us -> 0.64 us  [on_device(): doubled * 0.5]
    unnamed x2 -> x0, local copies, waits for them, and re-layouts: 0.6 us -> none
where the time goes in v1:
time: 43.9 us; the launch traced here: 43.7 us
  Pallas kernels  41.3 us (94%)
  between operations  1.29 us (3%)
  other arithmetic  1.15 us (3%)
    pallas_call x1, Pallas kernels, on_device(): pl.pallas_call(functools.partial(kernel, coils, frames), out_shape=(pltpu...  41.3 us

profile of v1, /device:TPU:0, one launch (start us, length us, event | category | flops | bytes accessed | tf_op | source)
XLA Modules:
  0.0 43.7 jit_solution(6032834120859964131)
XLA Ops:
  1.3 41.3 %shard_map.122 = (f32[128,128]{1,0:T(8,128)S(1)}, f32[1,2]{1,0:T(1,128)S(1)}) custom-call(f32[32,1,2,256]{3,2,1,0:T(2,128)} %refs_0_.1, bf16[1,2,256,256]{3,2,1,0:T(8,128)(2,1)} %refs_1_.1, bf16[1,1,18,2,256]{4,3,2,1,0:T(2,128)(2,1)} %refs_2_.1, s32[1,1]{1,0:T(1,128)} %bitcast.10.refs_3_, s32[1,18]{1,0:T(1,128)} %refs_4_.1, s32[1,18]{1,0:T(1,128)} %refs_5_.1, ...), custom_call_target="tpu_custom_call" | custom-call | tf_op jit(solution)/shard_map/pallas_call | solution.py:449
  42.6 0.6 %broadcast_multiply_fusion = f32[128,128]{1,0:T(8,128)} fusion(f32[128,128]{1,0:T(8,128)S(1)} %get-tuple-element.4), kind=kLoop, calls=%fused_computation | loop fusion | flops 16384 | bytes 131072 | tf_op jit(solution)/shard_map/mul | solution.py:490
  43.2 0.5 %multiply_bitcast_fusion = f32[2,1]{0,1:T(1,128)} fusion(f32[1,2]{1,0:T(1,128)S(1)} %get-tuple-element.5), kind=kLoop, calls=%fused_computation.1 | loop fusion | flops 2 | bytes 16 | tf_op jit(solution)/shard_map/transpose | solution.py:492

commit v2 on v1

--- a/solution.py
+++ b/solution.py
@@ -15,6 +15,8 @@
 TILE = 128
 ALIGN = 16
 LANES = 128
+LEAD = 3
+HOLD = (0, 1, 2, )
 
 step_size = 2.0
 tv_weight = 0.1
@@ -159,6 +161,7 @@
     beside_recv,
     tally_send,
     tally_recv,
+    turn_sem,
 ):
     coil = lax.axis_index("coil")
     frame = lax.axis_index("frame")
@@ -198,9 +201,35 @@
             device_id=where,
             device_id_type=MESH,
         )
-        copy.start()
         pending.append(copy)
         return copy
+
+    paired = frames % 2 == 0
+    sibling = frame + 1 - 2 * lax.rem(frame, 2)
+    first_core = lax.rem(frame, 2) == 0
+
+    def start(phase, copies):
+        if paired and phase in HOLD:
+            pl.when(jnp.logical_not(first_core))(lambda: pl.semaphore_wait(turn_sem.at[phase], 1))
+        for copy in copies:
+            copy.start()
+
+    def sent(phase, copies):
+        if paired and phase in HOLD:
+            for copy in copies:
+                pending[:] = [one for one in pending if one is not copy]
+
+            @pl.when(first_core)
+            def _():
+                for copy in copies[:LEAD]:
+                    copy.wait_send()
+                pl.semaphore_signal(turn_sem.at[phase], inc=1, device_id={"frame": sibling}, device_id_type=MESH)
+                for copy in copies[LEAD:]:
+                    copy.wait_send()
+
+            held_back.extend(copies)
+
+    held_back = []
 
     def spread_image(it, low, full):
         gathers = {
@@ -214,6 +243,7 @@
         return gathers, besides
 
     gathers, besides = spread_image(0, low_ref.at[0], moving_ref.at[0])
+    start(0, list(gathers.values()) + besides)
 
     for place in range(4, 10):
         loads[place].wait()
@@ -261,6 +291,7 @@
     deep = window * ALIGN
     for place in range(1, 4):
         loads[place].wait()
+    sent(0, list(gathers.values()))
     used = used_ref[0, 0]
     momentum = 1.0
 
@@ -316,8 +347,9 @@
                 rows_wide = row_ref[block, :strips].reshape(size, spoke)
                 for p in range(2):
                     left[p].append(lows[2 * member + p].astype(BF16) * rows_wide)
-            both = jnp.concatenate([jnp.concatenate(part, axis=1) for part in left], axis=0)
-            grid_ref[...] += dot_nt(both, jnp.concatenate(sides, axis=1))
+            side = jnp.concatenate(sides, axis=1)
+            for p in range(2):
+                grid_ref[p * size : (p + 1) * size] += dot_nt(jnp.concatenate(left[p], axis=1), side)
 
         def visit(turn, carry):
             total, lows = carry
@@ -329,12 +361,6 @@
         total, lows = lax.fori_loop(1, turns, visit, carry) if turns > 1 else carry
         spread(turns - 1, lows)
         tally_ref[it : it + 1, :] = total
-        tally_copies = []
-        if it == ITERS - 1:
-            tally_copies = [
-                send(tally_ref, tallies_ref.at[k], tally_send.at[k], tally_recv.at[k], {"coil": peers[k]})
-                for k in range(1, coils)
-            ]
         grid_real = grid_ref[:size].astype(BF16)
         grid_imag = grid_ref[size:].astype(BF16)
         turned = jnp.concatenate(
@@ -364,6 +390,15 @@
                 income_recv.at[it, k],
                 {"coil": peers[k]},
             )
+        start(2 * it + 1, incomes.values())
+        tally_copies = []
+        if it == ITERS - 1:
+            tally_copies = [
+                send(tally_ref, tallies_ref.at[k], tally_send.at[k], tally_recv.at[k], {"coil": peers[k]})
+                for k in range(1, coils)
+            ]
+            for copy in tally_copies:
+                copy.start()
         grad_ref[0] = real
         grad_ref[1] = imag
 
@@ -377,6 +412,7 @@
         behind_length = jnp.sqrt(behind[0] * behind[0] + behind[1] * behind[1] + floor)
         variation = [behind[p] / behind_length - ahead[p] / ahead_length for p in range(2)]
 
+        sent(2 * it + 1, list(incomes.values()))
         here = pl.multiple_of(coil * rows, rows)
         sums = [grad_ref[p, pl.ds(here, rows), :] for p in range(2)]
         for k in range(1, coils):
@@ -403,6 +439,8 @@
                 moving_ref[it + 1, p] = ahead_value
                 current_ref[p] = updated[p]
             gathers, besides = spread_image(it + 1, low_ref.at[it + 1], moving_ref.at[it + 1])
+            start(2 * it + 2, list(gathers.values()) + besides)
+            sent(2 * it + 2, list(gathers.values()))
         momentum = following
 
     tally = tally_ref[...]
@@ -416,6 +454,12 @@
     misfit_ref[...] = misfit
     for copy in pending:
         copy.wait_send()
+    if held_back:
+
+        @pl.when(jnp.logical_not(first_core))
+        def _():
+            for copy in held_back:
+                copy.wait_send()
 
 
 def on_device(coils, frames, table, image, coil_maps, samples, blocks_used, row_off, col_off, row_first, col_first, *taps):
@@ -482,6 +526,7 @@
             dma((ITERS, 2)),
             dma((coils,)),
             dma((coils,)),
+            pltpu.SemaphoreType.REGULAR((2 * ITERS,)),
         ],
         compiler_params=pltpu.CompilerParams(
             collective_id=0, has_side_effects=True, vmem_limit_bytes=56 * 1024 * 1024

time: 43.9 us -> 41.7 us (0.950)
  the two profiles are of different devices: /device:TPU:0 before, /device:TPU:1 now
where the time goes in v2:
time: 41.7 us; the launch traced here: 41.6 us
  Pallas kernels  39.1 us (94%)
  between operations  1.29 us (3%)
  other arithmetic  1.15 us (3%)
    pallas_call x1, Pallas kernels, on_device(): pl.pallas_call(functools.partial(kernel, coils, frames), out_shape=(pltpu...  39.1 us

profile of v2, /device:TPU:1, one launch (start us, length us, event | category | flops | bytes accessed | tf_op | source)
XLA Modules:
  0.0 41.6 jit_solution(10242611867345711016)
XLA Ops:
  1.3 39.1 %shard_map.122 = (f32[128,128]{1,0:T(8,128)S(1)}, f32[1,2]{1,0:T(1,128)S(1)}) custom-call(f32[32,1,2,256]{3,2,1,0:T(2,128)} %refs_0_.1, bf16[1,2,256,256]{3,2,1,0:T(8,128)(2,1)} %refs_1_.1, bf16[1,1,18,2,256]{4,3,2,1,0:T(2,128)(2,1)} %refs_2_.1, s32[1,1]{1,0:T(1,128)} %bitcast.10.refs_3_, s32[1,18]{1,0:T(1,128)} %refs_4_.1, s32[1,18]{1,0:T(1,128)} %refs_5_.1, ...), custom_call_target="tpu_custom_call" | custom-call | tf_op jit(solution)/shard_map/pallas_call | solution.py:493
  40.4 0.6 %broadcast_multiply_fusion = f32[128,128]{1,0:T(8,128)} fusion(f32[128,128]{1,0:T(8,128)S(1)} %get-tuple-element.4), kind=kLoop, calls=%fused_computation | loop fusion | flops 16384 | bytes 131072 | tf_op jit(solution)/shard_map/mul | solution.py:535
  41.0 0.5 %multiply_bitcast_fusion = f32[2,1]{0,1:T(1,128)} fusion(f32[1,2]{1,0:T(1,128)S(1)} %get-tuple-element.5), kind=kLoop, calls=%fused_computation.1 | loop fusion | flops 2 | bytes 16 | tf_op jit(solution)/shard_map/transpose | solution.py:537

commit v3 on v2

--- a/solution.py
+++ b/solution.py
@@ -15,8 +15,7 @@
 TILE = 128
 ALIGN = 16
 LANES = 128
-LEAD = 3
-HOLD = (0, 1, 2, )
+HOLD = {0: 7, 1: 3, 2: 3}
 
 step_size = 2.0
 tv_weight = 0.1
@@ -176,6 +175,8 @@
     owners = [owner_of(coil, k, coils) for k in range(coils)]
     order = list(range(coils - 1, 0, -1))
     wire = gather_ref.dtype
+    halved = coils & (coils - 1) == 0 and coils > 1
+    top = coil // max(coils // 2, 1)
 
     barrier = pltpu.get_barrier_semaphore()
     for k in range(1, coils):
@@ -221,10 +222,10 @@
 
             @pl.when(first_core)
             def _():
-                for copy in copies[:LEAD]:
+                for copy in copies[: HOLD[phase]]:
                     copy.wait_send()
                 pl.semaphore_signal(turn_sem.at[phase], inc=1, device_id={"frame": sibling}, device_id_type=MESH)
-                for copy in copies[LEAD:]:
+                for copy in copies[HOLD[phase] :]:
                     copy.wait_send()
 
             held_back.extend(copies)
@@ -314,10 +315,13 @@
             stack_ref[pl.ds(at, rows), size:] = imag
             stack_ref[pl.ds(at_below, rows), :size] = imag
             stack_ref[pl.ds(at_below, rows), size:] = -real
-        half = dot(table_ref[...], stack_ref[...].astype(BF16)).astype(BF16)
-        kspace = dot(half, forward_ref[...]).astype(BF16)
+        half = jnp.concatenate(
+            [dot(table_ref[...], stack_ref[:, p * size : (p + 1) * size].astype(BF16)).astype(BF16) for p in range(2)],
+            axis=1,
+        )
         for p in range(2):
-            space_ref[p, :strips] = kspace[:, p * size : (p + 1) * size].reshape(strips, ALIGN, size)
+            kspace = dot(half, forward_ref[:, p * size : (p + 1) * size]).astype(BF16)
+            space_ref[p, :strips] = kspace.reshape(strips, ALIGN, size)
         grid_ref[...] = jnp.zeros_like(grid_ref)
 
         def predict(turn, total):
@@ -370,27 +374,36 @@
             ],
             axis=0,
         )
-        back_half = dot(table_ref[...], turned).astype(BF16)
-        coil_back = dot(back_half, inverse_ref[...])
-        map_real = maps_ref[0, 0].astype(F32)
-        map_imag = maps_ref[0, 1].astype(F32)
-        back_real = coil_back[:, :size]
-        back_imag = coil_back[:, size:]
-        real = map_real * back_real + map_imag * back_imag
-        imag = map_real * back_imag - map_imag * back_real
-        outgo_ref[it, 0] = real.astype(wire)
-        outgo_ref[it, 1] = imag.astype(wire)
         incomes = {}
-        for k in order:
-            at = pl.multiple_of(peers[k] * rows, rows)
-            incomes[k] = send(
-                outgo_ref.at[it, :, pl.ds(at, rows), :],
-                income_ref.at[it, k],
-                income_send.at[it, k],
-                income_recv.at[it, k],
-                {"coil": peers[k]},
-            )
-        start(2 * it + 1, incomes.values())
+        share = size // 2 if halved else size
+        for step in range(size // share):
+            low = pl.multiple_of((top if step else 1 - top) * share, share) if halved else 0
+            span = pl.ds(low, share)
+            back_half = dot(table_ref[span, :], turned).astype(BF16)
+            coil_back = dot(back_half, inverse_ref[...])
+            map_real = maps_ref[0, 0, span, :].astype(F32)
+            map_imag = maps_ref[0, 1, span, :].astype(F32)
+            back_real = coil_back[:, :size]
+            back_imag = coil_back[:, size:]
+            grad = (map_real * back_real + map_imag * back_imag, map_real * back_imag - map_imag * back_real)
+            for p in range(2):
+                outgo_ref[it, p, span, :] = grad[p].astype(wire)
+                grad_ref[p, span, :] = grad[p]
+            members = order if not halved else [k for k in order if (k < coils // 2) == (step == 1)]
+            for k in members:
+                at = pl.multiple_of(peers[k] * rows, rows)
+                incomes[k] = send(
+                    outgo_ref.at[it, :, pl.ds(at, rows), :],
+                    income_ref.at[it, k],
+                    income_send.at[it, k],
+                    income_recv.at[it, k],
+                    {"coil": peers[k]},
+                )
+            if step == 0:
+                start(2 * it + 1, [incomes[k] for k in members])
+            else:
+                for k in members:
+                    incomes[k].start()
         tally_copies = []
         if it == ITERS - 1:
             tally_copies = [
@@ -399,8 +412,6 @@
             ]
             for copy in tally_copies:
                 copy.start()
-        grad_ref[0] = real
-        grad_ref[1] = imag
 
         for copy in besides:
             copy.wait_recv()

time: 41.7 us -> 41.4 us (level)
  no operation moved by 1% of the time
where the time goes in v3:
time: 41.4 us; the launch traced here: 41.2 us
  Pallas kernels  38.8 us (94%)
  between operations  1.29 us (3%)
  other arithmetic  1.15 us (3%)
    pallas_call x1, Pallas kernels, on_device(): pl.pallas_call(functools.partial(kernel, coils, frames), out_shape=(pltpu...  38.8 us

profile of v3, /device:TPU:1, one launch (start us, length us, event | category | flops | bytes accessed | tf_op | source)
XLA Modules:
  0.0 41.2 jit_solution(8747885225575160240)
XLA Ops:
  1.3 38.8 %shard_map.122 = (f32[128,128]{1,0:T(8,128)S(1)}, f32[1,2]{1,0:T(1,128)S(1)}) custom-call(f32[32,1,2,256]{3,2,1,0:T(2,128)} %refs_0_.1, bf16[1,2,256,256]{3,2,1,0:T(8,128)(2,1)} %refs_1_.1, bf16[1,1,18,2,256]{4,3,2,1,0:T(2,128)(2,1)} %refs_2_.1, s32[1,1]{1,0:T(1,128)} %bitcast.10.refs_3_, s32[1,18]{1,0:T(1,128)} %refs_4_.1, s32[1,18]{1,0:T(1,128)} %refs_5_.1, ...), custom_call_target="tpu_custom_call" | custom-call | tf_op jit(solution)/shard_map/pallas_call | solution.py:504
  40.1 0.6 %broadcast_multiply_fusion = f32[128,128]{1,0:T(8,128)} fusion(f32[128,128]{1,0:T(8,128)S(1)} %get-tuple-element.4), kind=kLoop, calls=%fused_computation | loop fusion | flops 16384 | bytes 131072 | tf_op jit(solution)/shard_map/mul | solution.py:546
  40.7 0.5 %multiply_bitcast_fusion = f32[2,1]{0,1:T(1,128)} fusion(f32[1,2]{1,0:T(1,128)S(1)} %get-tuple-element.5), kind=kLoop, calls=%fused_computation.1 | loop fusion | flops 2 | bytes 16 | tf_op jit(solution)/shard_map/transpose | solution.py:548

commit v4 on v3

--- a/solution.py
+++ b/solution.py
@@ -543,9 +543,19 @@
             collective_id=0, has_side_effects=True, vmem_limit_bytes=56 * 1024 * 1024
         ),
     )(*operands)
-    updated = (doubled * 0.5).reshape(rows, size // LANES, 2, LANES).transpose(0, 2, 1, 3)
-    scale = 0.5 / (coils * blocks * spoke)
-    return updated.reshape(image.shape), jnp.transpose(misfit * scale)
+
+    def finish(doubled_ref, sums_ref, image_ref, misfit_ref):
+        image_ref[...] = doubled_ref[...] * 0.5
+        misfit_ref[...] = sums_ref[...] * (0.5 / (coils * blocks * spoke))
+
+    doubled, misfit = pl.pallas_call(
+        finish,
+        out_shape=(jax.ShapeDtypeStruct(doubled.shape, F32), jax.ShapeDtypeStruct(misfit.shape, F32)),
+        in_specs=[vmem, vmem],
+        out_specs=(vmem, vmem),
+    )(pltpu.with_memory_space_constraint(doubled, pltpu.VMEM), pltpu.with_memory_space_constraint(misfit, pltpu.VMEM))
+    updated = doubled.reshape(rows, size // LANES, 2, LANES).transpose(0, 2, 1, 3)
+    return updated.reshape(image.shape), jnp.transpose(misfit)
 
 
 def solution(mesh):

time: 41.4 us -> 40.9 us (0.988)
  other arithmetic: 1.15 us -> 0 us
  Pallas kernels: 38.8 us -> 39.5 us
    pallas_call x0 -> x1, Pallas kernels: none -> 0.64 us  [on_device(): pl.pallas_call(finish, out_shape=(jax.ShapeDtypeStruct(doubled.shape, F32...]
    mul x1 -> x0, other arithmetic: 0.64 us -> none  [on_device(): doubled * 0.5]
    transpose x1 -> x0, other arithmetic: 0.51 us -> none  [on_device(): return (updated.reshape(image.shape), jnp.transpose(misfit * scale))]
where the time goes in v4:
time: 40.9 us; the launch traced here: 40.8 us
  Pallas kernels  39.5 us (97%)
  between operations  1.29 us (3%)
    pallas_call x1, Pallas kernels, on_device(): pl.pallas_call(functools.partial(kernel, coils, frames), out_shape=(pltpu...  38.8 us

profile of v4, /device:TPU:1, one launch (start us, length us, event | category | flops | bytes accessed | tf_op | source)
XLA Modules:
  0.0 40.8 jit_solution(10524779686839551632)
XLA Ops:
  1.3 38.8 %shard_map.122 = (f32[128,128]{1,0:T(8,128)S(1)}, f32[1,2]{1,0:T(1,128)S(1)}) custom-call(f32[32,1,2,256]{3,2,1,0:T(2,128)} %refs_0_.1, bf16[1,2,256,256]{3,2,1,0:T(8,128)(2,1)} %refs_1_.1, bf16[1,1,18,2,256]{4,3,2,1,0:T(2,128)(2,1)} %refs_2_.1, s32[1,1]{1,0:T(1,128)} %bitcast.9.refs_3_, s32[1,18]{1,0:T(1,128)} %refs_4_.1, s32[1,18]{1,0:T(1,128)} %refs_5_.1, ...), custom_call_target="tpu_custom_call" | custom-call | tf_op jit(solution)/shard_map/pallas_call | solution.py:504
  40.1 0.6 %shard_map.123 = (f32[128,128]{1,0:T(8,128)}, f32[1,2]{1,0:T(1,128)}) custom-call(f32[128,128]{1,0:T(8,128)S(1)} %get-tuple-element.6.doubled_ref, f32[1,2]{1,0:T(1,128)S(1)} %get-tuple-element.7.sums_ref), custom_call_target="tpu_custom_call" | custom-call | tf_op jit(solution)/shard_map/pallas_call | solution.py:551

commit v5 on v4

--- a/solution.py
+++ b/solution.py
@@ -15,7 +15,7 @@
 TILE = 128
 ALIGN = 16
 LANES = 128
-HOLD = {0: 7, 1: 3, 2: 3}
+HOLD = {0: 7, 1: 3, 2: 4}
 
 step_size = 2.0
 tv_weight = 0.1

time: 40.9 us -> 40.9 us (level)
  no operation moved by 1% of the time
where the time goes in v5:
time: 40.9 us; the launch traced here: 40.7 us
  Pallas kernels  39.5 us (97%)
  between operations  1.29 us (3%)
    pallas_call x1, Pallas kernels, on_device(): pl.pallas_call(functools.partial(kernel, coils, frames), out_shape=(pltpu...  38.8 us

profile of v5, /device:TPU:1, one launch (start us, length us, event | category | flops | bytes accessed | tf_op | source)
XLA Modules:
  0.0 40.7 jit_solution(2982909378243702566)
XLA Ops:
  1.3 38.8 %shard_map.122 = (f32[128,128]{1,0:T(8,128)S(1)}, f32[1,2]{1,0:T(1,128)S(1)}) custom-call(f32[32,1,2,256]{3,2,1,0:T(2,128)} %refs_0_.1, bf16[1,2,256,256]{3,2,1,0:T(8,128)(2,1)} %refs_1_.1, bf16[1,1,18,2,256]{4,3,2,1,0:T(2,128)(2,1)} %refs_2_.1, s32[1,1]{1,0:T(1,128)} %bitcast.9.refs_3_, s32[1,18]{1,0:T(1,128)} %refs_4_.1, s32[1,18]{1,0:T(1,128)} %refs_5_.1, ...), custom_call_target="tpu_custom_call" | custom-call | tf_op jit(solution)/shard_map/pallas_call | solution.py:504
  40.1 0.6 %shard_map.123 = (f32[128,128]{1,0:T(8,128)}, f32[1,2]{1,0:T(1,128)}) custom-call(f32[128,128]{1,0:T(8,128)S(1)} %get-tuple-element.6.doubled_ref, f32[1,2]{1,0:T(1,128)S(1)} %get-tuple-element.7.sums_ref), custom_call_target="tpu_custom_call" | custom-call | tf_op jit(solution)/shard_map/pallas_call | solution.py:551
